TPU v7x, 32 devices: a whole 2x2x4 slice. The times are simulated.
32 devices in a mesh: section: 2 (over x), dp: 16 (over z, y, core).
Axes of the slice: x: 2, y: 2, z: 4, core: 2. Of those that a mesh axis runs over, the one named last changes fastest.
Arguments:
- features: bfloat16 [1, 2, 2048, 4096], P(None, 'section', 'dp'), parts along dimension 2, may hold values from -6 to 6
- in_proj: bfloat16 [2, 4096, 512], P('section'), may hold values from -0.09375 to 0.09375
- mix_proj: bfloat16 [2, 2, 256, 256], P('section'), may hold values from -0.375 to 0.375
- out_proj: bfloat16 [2, 512, 4096], P('section'), may hold values from -0.375 to 0.375
- gate_proj: bfloat16 [2, 2, 4096], P('section'), may hold values from -0.09375 to 0.09375
- cross_bias: float32 [2, 4096], P('section'), may hold values from -3 to 3
Outputs:
- crossed: bfloat16 [1, 2, 2048, 4096], P(None, 'section', 'dp'), parts along dimension 2
There are 16 independent parts, one for each index of `dp`. A program takes and returns all parts, laid end to end along the dimension named above; an argument that names none is the same for every part. Nothing has to cross between parts.
All inputs are finite; a program needn't handle non-finite values.
Results may differ from a plain program's by a relative error of at most 0.015.
Values may be sent and summed in bfloat16 or wider, within the bound.
A program may use at most 64 MiB of HBM per device.

v0:
```python
import jax
import jax.numpy as jnp
from jax import lax
from jax.sharding import PartitionSpec as P


def from_behind(block, axis, distance):
    devices = range(lax.axis_size(axis))
    route = [(i - distance, i) for i in devices if i - distance in devices]
    return lax.ppermute(block, axis, route)


def cross_layer(current, anchor, v_mat, c_mat, u_mat, gate_mat, shift_row):
    row_count = current.shape[0]
    expert_count = c_mat.shape[0]
    rank_size = c_mat.shape[1]
    projected = jnp.dot(current, v_mat, preferred_element_type=jnp.float32)
    inner_first = (
        jnp.tanh(projected).astype(jnp.bfloat16).reshape(row_count, expert_count, rank_size)
    )
    inner_second = jnp.einsum(
        "rek,ekj->rej", inner_first, c_mat, preferred_element_type=jnp.float32
    )
    logits = lax.dot_general(
        current, gate_mat, (((1,), (1,)), ((), ())), preferred_element_type=jnp.float32
    )
    gate_values = 1.0 / jnp.sum(jnp.exp(logits[:, None, :] - logits[:, :, None]), axis=2)
    blended = (gate_values[:, :, None] * jnp.tanh(inner_second)).astype(jnp.bfloat16)
    blended = blended.reshape(row_count, expert_count * rank_size)
    crossed = jnp.dot(blended, u_mat, preferred_element_type=jnp.float32)
    updated = current.astype(jnp.float32) + anchor.astype(jnp.float32) * (crossed + shift_row)
    return updated.astype(jnp.bfloat16)


def per_device(features, in_proj, mix_proj, out_proj, gate_proj, cross_bias):
    section_count = lax.axis_size("section")
    position = lax.axis_index("section")
    pieces = 1
    local_micro = features.shape[0]
    row_count = features.shape[2]
    feature_count = features.shape[3]
    piece_rows = row_count // pieces
    everyone = lax.all_gather(features, "section", axis=1, tiled=True)
    all_units = everyone.reshape(local_micro * section_count * pieces, piece_rows, feature_count)
    unit_count = all_units.shape[0]
    step_count = unit_count + section_count - 1
    v_mat = in_proj[0]
    c_mat = mix_proj[0]
    u_mat = out_proj[0]
    gate_mat = gate_proj[0]
    shift_row = cross_bias[0]

    def apply_layer(current, anchor):
        return cross_layer(current, anchor, v_mat, c_mat, u_mat, gate_mat, shift_row)

    def keep_input(current, anchor):
        return current

    def advance(carried, moment):
        incoming, outgoing, collected = carried
        unit_here = moment - position
        active = (unit_here >= 0) & (unit_here < unit_count)
        anchor = lax.dynamic_index_in_dim(
            all_units, jnp.clip(unit_here, 0, unit_count - 1), 0, keepdims=False
        )
        current = jnp.where(position == 0, anchor, incoming)
        result = lax.cond(active, apply_layer, keep_input, current, anchor)
        outgoing = jnp.where(position == section_count - 1, result, outgoing)
        held_unit = moment + position - 2 * section_count + 2
        arrived = (
            (held_unit >= 0)
            & (held_unit < unit_count)
            & (held_unit // pieces % section_count == position)
        )
        held_safe = jnp.clip(held_unit, 0, unit_count - 1)
        slot_index = held_safe // pieces // section_count * pieces + held_safe % pieces
        previous = lax.dynamic_index_in_dim(collected, slot_index, 0, keepdims=False)
        collected = lax.dynamic_update_index_in_dim(
            collected, jnp.where(arrived, outgoing, previous), slot_index, 0
        )
        return (result, outgoing, collected)

    def forward_step(carried, moment):
        result, outgoing, collected = advance(carried, moment)
        incoming = from_behind(result, "section", 1)
        return ((incoming, outgoing, collected), None)

    def cycle_step(carried, moment):
        moved, _ = forward_step(carried, moment)
        incoming, outgoing, collected = moved
        outgoing = from_behind(outgoing, "section", -1)
        return ((incoming, outgoing, collected), None)

    blank = jnp.zeros((piece_rows, feature_count), jnp.bfloat16)
    holding = jnp.zeros((local_micro * pieces, piece_rows, feature_count), jnp.bfloat16)
    carried, _ = lax.scan(
        forward_step, (blank, blank, holding), jnp.arange(0, section_count - 1, dtype=jnp.int32)
    )
    carried, _ = lax.scan(
        cycle_step, carried, jnp.arange(section_count - 1, step_count - 1, dtype=jnp.int32)
    )
    _, _, collected = advance(carried, jnp.int32(step_count - 1))
    return collected.reshape(local_micro, 1, row_count, feature_count)


def solution(mesh):
    placed = (
        P(None, "section", "dp", None),
        P("section", None, None),
        P("section", None, None, None),
        P("section", None, None),
        P("section", None, None),
        P("section", None),
    )
    return jax.shard_map(
        per_device,
        mesh=mesh,
        in_specs=placed,
        out_specs=P(None, "section", "dp", None),
        check_vma=False,
    )
```

profile of v0, /device:TPU:18, one launch (start us, length us, event | category | flops | bytes accessed | tf_op | source)
XLA Modules:
  0.0 130.2 jit_solution(13214571090702250396)
XLA Ops:
  6.5 0.7 all-gather.2.cloned.1.call-update
  7.3 34.9 %all-gather.2.cloned.1.call-done = bf16[1,2,128,4096]{3,2,0,1:T(8,128)(2,1)} async-done(((bf16[1,1,128,4096]{3,2,0,1:T(8,128)(2,1)}), bf16[1,2,128,4096]{3,2,0,1:T(8,128)(2,1)}) %all-gather.2.cloned.1.call-update) | async-done | bytes 2097168 | tf_op jit(solution)/shard_map/all_gather | solution.py:43
  42.1 1.4 %broadcast_select_fusion.2 = (bf16[128,4096]{1,0:T(8,128)(2,1)S(1)}, bf16[128,4096]{1,0:T(8,128)(2,1)S(1)}) fusion(pred[]{:T(512)S(6)} %eq.38, bf16[1,2,128,4096]{3,2,0,1:T(8,128)(2,1)} %all-gather.2.cloned.1.call-done, s32[]{:T(128)S(6)} %min.19), kind=kLoop, calls=%fused_computation.48 | loop fusion | flops 524288 | bytes 3145733 | tf_op jit(solution)/shard_map/while/body/eval_jaxpr/jit(_where)/select_n | solution.py:66
  43.5 1.3 collective-permute-start
  44.8 31.8 %collective-permute-done = bf16[128,4096]{1,0:T(8,128)(2,1)} collective-permute-done((bf16[128,4096]{1,0:T(8,128)(2,1)S(1)}, bf16[128,4096]{1,0:T(8,128)(2,1)}, u32[]{:S(2)}, u32[]{:S(2)}) %collective-permute-start) | collective-permute-done | bytes 1048608 | tf_op jit(solution)/shard_map/while/body/eval_jaxpr/ppermute | solution.py:10
  76.7 1.7 %broadcast_select_fusion.1 = (bf16[128,4096]{1,0:T(8,128)(2,1)S(1)}, bf16[128,4096]{1,0:T(8,128)(2,1)S(1)}) fusion(bf16[128,4096]{1,0:T(8,128)(2,1)} %collective-permute-done, pred[]{:T(512)S(6)} %eq.38, bf16[1,2,128,4096]{3,2,0,1:T(8,128)(2,1)} %all-gather.2.cloned.1.call-done, s32[]{:T(128)S(6)} %min.18), kind=kLoop, calls=%fused_computation.47 | loop fusion | flops 524288 | bytes 4194309 | tf_op jit(solution)/shard_map/while/body/eval_jaxpr/jit(_where)/select_n | solution.py:66
  78.4 7.4 %conditional.4 = (bf16[128,4096]{1,0:T(8,128)(2,1)S(1)}) conditional(s32[]{:T(128)} %convert_element_type.57, bf16[128,4096]{1,0:T(8,128)(2,1)S(1)} %get-tuple-element.150, (bf16[128,4096]{1,0:T(8,128)(2,1)S(1)}, bf16[128,4096]{1,0:T(8,128)(2,1)S(1)}, bf16[2,4096]{1,0:T(2,128)(2,1)S(1)}, bf16[4096,512]{1,0:T(8,128)(2,1)}, ...), branch_computations={%region_3.4_spmd, %region_4.6_spmd} | conditional | flops 1112736768 | bytes 15767588 | solution.py:67
  78.4 3.0 %fusion.14 = bf16[128,512]{1,0:T(8,128)(2,1)S(1)} fusion(bf16[128,4096]{1,0:T(8,128)(2,1)S(1)} %get-tuple-element.134, bf16[4096,512]{1,0:T(8,128)(2,1)} %get-tuple-element.137), kind=kOutput, calls=%fused_computation.22 | convolution fusion | flops 536936448 | bytes 5373952 | tf_op jit(solution)/shard_map/while/body/eval_jaxpr/cond/branch_1_fun/dot_general | solution.py:17
  81.3 0.4 fusion.28
  81.8 0.2 fusion.15
  82.0 0.1 copy.44
  82.1 3.6 %fusion.11 = bf16[128,4096]{1,0:T(8,128)(2,1)S(1)} fusion(bf16[128,512]{0,1:T(8,128)(2,1)S(1)} %bitcast.81, bf16[512,4096]{1,0:T(8,128)(2,1)} %get-tuple-element.139, bf16[128,4096]{1,0:T(8,128)(2,1)S(1)} %get-tuple-element.135, bf16[128,4096]{1,0:T(8,128)(2,1)S(1)} %get-tuple-element.134, f32[4096]{0:T(1024)S(1)} %bitcast.87), kind=kOutput, calls=%fused_computation.17 | convolution fusion | flops 540016640 | bytes 7487488 | tf_op jit(solution)/shard_map/while/body/eval_jaxpr/cond/branch_1_fun/dot_general | solution.py:30
  85.7 1.3 collective-permute-start.1
  87.0 1.1 broadcast_select_fusion.3
  88.1 6.5 %collective-permute-start.2 = (bf16[128,4096]{1,0:T(8,128)(2,1)}, bf16[128,4096]{1,0:T(8,128)(2,1)}, u32[]{:S(2)}, u32[]{:S(2)}) collective-permute-start(bf16[128,4096]{1,0:T(8,128)(2,1)} %broadcast_select_fusion.3), channel_id=1, source_target_pairs={{16,0},{17,1},{18,2},{19,3},{20,4},{21,5},{22,6},{23,7},{24,8},{25... | collective-permute-start | bytes 3145736 | tf_op jit(solution)/shard_map/while/body/eval_jaxpr/ppermute | solution.py:10
  94.6 17.3 %collective-permute-done.1 = bf16[128,4096]{1,0:T(8,128)(2,1)} collective-permute-done((bf16[128,4096]{1,0:T(8,128)(2,1)S(1)}, bf16[128,4096]{1,0:T(8,128)(2,1)}, u32[]{:S(2)}, u32[]{:S(2)}) %collective-permute-start.1) | collective-permute-done | bytes 1048608 | tf_op jit(solution)/shard_map/while/body/eval_jaxpr/ppermute | solution.py:10
  111.9 2.6 %broadcast_select_fusion = (bf16[128,4096]{1,0:T(8,128)(2,1)S(1)}, bf16[128,4096]{1,0:T(8,128)(2,1)}) fusion(bf16[128,4096]{1,0:T(8,128)(2,1)} %collective-permute-done.1, pred[]{:T(512)S(6)} %eq.38, bf16[1,2,128,4096]{3,2,0,1:T(8,128)(2,1)} %all-gather.2.cloned.1.call-done, s32[]{:T(128)S(6)} %min.17), kind=kLoop, calls=%fused_computation.46 | loop fusion | flops 524288 | bytes 4194309 | tf_op jit(solution)/shard_map/jit(_where)/select_n | solution.py:66
  114.5 7.6 %conditional.5 = (bf16[128,4096]{1,0:T(8,128)(2,1)S(1)}) conditional(s32[]{:T(128)} %convert_element_type.56, bf16[128,4096]{1,0:T(8,128)(2,1)S(1)} %get-tuple-element.148, (bf16[128,4096]{1,0:T(8,128)(2,1)S(1)}, bf16[128,4096]{1,0:T(8,128)(2,1)}, bf16[2,4096]{1,0:T(2,128)(2,1)S(1)}, bf16[4096,512]{1,0:T(8,128)(2,1)}, bf16[2,256,256]{2,1,0:T(8,128)(2,1)}, ...), branch_computations={%region_6.7_spmd, %region_7.9_spmd} | conditional | flops 1112736768 | bytes 15767588 | solution.py:67
  114.5 3.0 %fusion.23 = bf16[128,512]{1,0:T(8,128)(2,1)S(1)} fusion(bf16[128,4096]{1,0:T(8,128)(2,1)S(1)} %get-tuple-element.141, bf16[4096,512]{1,0:T(8,128)(2,1)} %get-tuple-element.144), kind=kOutput, calls=%fused_computation.36 | convolution fusion | flops 536936448 | bytes 5373952 | tf_op jit(solution)/shard_map/cond/branch_1_fun/dot_general | solution.py:17
  117.5 0.4 fusion.29
  117.9 0.2 fusion.24
  118.1 0.1 copy.46
  118.3 3.9 %fusion.20 = bf16[128,4096]{1,0:T(8,128)(2,1)S(1)} fusion(bf16[128,512]{0,1:T(8,128)(2,1)S(1)} %bitcast.82, bf16[512,4096]{1,0:T(8,128)(2,1)} %get-tuple-element.146, bf16[128,4096]{1,0:T(8,128)(2,1)} %get-tuple-element.142, bf16[128,4096]{1,0:T(8,128)(2,1)S(1)} %get-tuple-element.141, f32[4096]{0:T(1024)S(1)} %bitcast.88), kind=kOutput, calls=%fused_computation.31 | convolution fusion | flops 540016640 | bytes 7487488 | tf_op jit(solution)/shard_map/cond/branch_1_fun/dot_general | solution.py:30
  122.2 1.2 select_bitcast_fusion
  (17 shorter events, 0.1 us)
Async XLA Ops:
  6.5 35.6 %all-gather.2.cloned.1.call-start = ((), (), s32[]{:S(2)}) async-start(), calls=%async_computation | async-start | bytes 3145728 | tf_op jit(solution)/shard_map/all_gather | solution.py:43
  6.5 37.0 %copy-start = (bf16[1,2,4096]{2,1,0:T(2,128)(2,1)S(1)}, bf16[1,2,4096]{2,1,0:T(2,128)(2,1)}, u32[]{:S(2)}) copy-start(bf16[1,2,4096]{2,1,0:T(2,128)(2,1)} %param.16) | copy-start | bytes 49156
  6.5 37.0 %copy-start.1 = (f32[1,4096]{1,0:T(1,128)S(1)}, f32[1,4096]{1,0:T(1,128)}, u32[]{:S(2)}) copy-start(f32[1,4096]{1,0:T(1,128)} %param.17) | copy-start | bytes 49156
  6.5 37.0 %copy-start.2 = (bf16[1,2,256,256]{3,2,1,0:T(8,128)(2,1)S(1)}, bf16[1,2,256,256]{3,2,1,0:T(8,128)(2,1)}, u32[]{:S(2)}) copy-start(bf16[1,2,256,256]{3,2,1,0:T(8,128)(2,1)} %param.14) | copy-start | bytes 786436
  43.5 33.1 %collective-permute-start = (bf16[128,4096]{1,0:T(8,128)(2,1)S(1)}, bf16[128,4096]{1,0:T(8,128)(2,1)}, u32[]{:S(2)}, u32[]{:S(2)}) collective-permute-start(bf16[128,4096]{1,0:T(8,128)(2,1)S(1)} %get-tuple-element.154), channel_id=1, source_target_pairs={{0,16},{1,17},{2,18},{3,19},{4,20},{5,21},{6,22},{7,23},{8,24},{9,... | collective-permute-start | bytes 3145736 | tf_op jit(solution)/shard_map/while/body/eval_jaxpr/ppermute | solution.py:10
  78.4 3.4 %copy-start.3 = (bf16[2,256,256]{2,1,0:T(8,128)(2,1)S(1)}, bf16[2,256,256]{2,1,0:T(8,128)(2,1)}, u32[]{:S(2)}) copy-start(bf16[2,256,256]{2,1,0:T(8,128)(2,1)} %get-tuple-element.138) | copy-start | bytes 786436 | tf_op jit(solution)/shard_map/while/body/eval_jaxpr/cond
  85.7 26.2 %collective-permute-start.1 = (bf16[128,4096]{1,0:T(8,128)(2,1)S(1)}, bf16[128,4096]{1,0:T(8,128)(2,1)}, u32[]{:S(2)}, u32[]{:S(2)}) collective-permute-start(bf16[128,4096]{1,0:T(8,128)(2,1)S(1)} %get-tuple-element.155), channel_id=1, source_target_pairs={{0,16},{1,17},{2,18},{3,19},{4,20},{5,21},{6,22},{7,23},{8,24},{9,... | collective-permute-start | bytes 3145736 | tf_op jit(solution)/shard_map/while/body/eval_jaxpr/ppermute | solution.py:10
  88.1 34.0 %collective-permute-start.2 = (bf16[128,4096]{1,0:T(8,128)(2,1)}, bf16[128,4096]{1,0:T(8,128)(2,1)}, u32[]{:S(2)}, u32[]{:S(2)}) collective-permute-start(bf16[128,4096]{1,0:T(8,128)(2,1)} %broadcast_select_fusion.3), channel_id=1, source_target_pairs={{16,0},{17,1},{18,2},{19,3},{20,4},{21,5},{22,6},{23,7},{24,8},{25... | collective-permute-start | bytes 3145736 | tf_op jit(solution)/shard_map/while/body/eval_jaxpr/ppermute | solution.py:10
  114.5 3.4 %copy-start.4 = (bf16[2,256,256]{2,1,0:T(8,128)(2,1)S(1)}, bf16[2,256,256]{2,1,0:T(8,128)(2,1)}, u32[]{:S(2)}) copy-start(bf16[2,256,256]{2,1,0:T(8,128)(2,1)} %get-tuple-element.145) | copy-start | bytes 786436 | tf_op jit(solution)/shard_map/cond
Sparse Core Ops, SparseCore 0:
  8.9 33.2 all-gather.1
where the time goes:
time: 131 us; the launch traced here: 130 us
  waiting for transfers between devices  84.6 us (65%)
  matrix products  14.5 us (11%)
  between operations  13.5 us (10%)
  starting transfers between devices  9.1 us (7%)
  other arithmetic  8.06 us (6%)
    ppermute x3, waiting for transfers between devices, from_behind(): return lax.ppermute(block, axis, route)  49.1 us
    all_gather x1, waiting for transfers between devices, per_device(): everyone = lax.all_gather(features, 'section', axis=1, tiled=True)  34.9 us
    ppermute x3, starting transfers between devices, from_behind(): return lax.ppermute(block, axis, route)  9.1 us
    dot_general x2, matrix products, cross_layer(): crossed = jnp.dot(blended, u_mat, preferred_element_type=jnp.float32)  7.47 us
    dot_general x2, matrix products, cross_layer(): projected = jnp.dot(current, v_mat, preferred_element_type=jnp.float32)  5.92 us
    select_n x3, other arithmetic, advance(): current = jnp.where(position == 0, anchor, incoming)  5.69 us
  transfers between devices with their start and end apart: 4, of which 3 were waited for; matrix products, arithmetic and copies ran while one was open for 9% of the time, Pallas kernels for 0%

commit v1 on v0

--- a/solution.py
+++ b/solution.py
@@ -1,7 +1,212 @@
 import jax
+
 import jax.numpy as jnp
 from jax import lax
+from jax.experimental import pallas as pl
+from jax.experimental.pallas import tpu as pltpu
 from jax.sharding import PartitionSpec as P
+
+CHUNKS = 8
+
+
+def relay_kernel(
+    x_hbm, v_hbm, c_hbm, u_hbm, g_hbm, b_hbm, o_hbm,
+    xb, vb, cb, ub, gb, bb, in1, in2, out1, out2, ob, proj, lg, bl,
+    lx, lv, lu, lw, s1, r1, s2, r2, so,
+):
+    chunks, rows, width = xb.shape
+    experts, rank, _ = cb.shape
+    me = lax.axis_index("section")
+    peer = 1 - me
+
+    def columns(c):
+        return pl.ds(pl.multiple_of(c * width, width), width)
+
+    def load_x(c):
+        return pltpu.make_async_copy(x_hbm.at[:, columns(c)], xb.at[c], lx.at[c])
+
+    def load_v(c):
+        return pltpu.make_async_copy(v_hbm.at[columns(c)], vb.at[c], lv.at[c])
+
+    def load_u(c):
+        return pltpu.make_async_copy(u_hbm.at[:, columns(c)], ub.at[c], lu.at[c])
+
+    load_c = pltpu.make_async_copy(c_hbm, cb, lw.at[0])
+    load_g = pltpu.make_async_copy(g_hbm, gb, lw.at[1])
+    load_b = pltpu.make_async_copy(b_hbm, bb, lw.at[2])
+
+    def put(src, dst, send, recv, c):
+        return pltpu.make_async_remote_copy(
+            src_ref=src, dst_ref=dst.at[c], send_sem=send.at[c], recv_sem=recv.at[c],
+            device_id={"section": peer}, device_id_type=pl.DeviceIdType.MESH,
+        )
+
+    def put_out(c):
+        return pltpu.make_async_copy(ob.at[c], o_hbm.at[:, columns(c)], so.at[c])
+
+    def each(body):
+        def step(c, carry):
+            body(c)
+            return carry
+        lax.fori_loop(0, chunks, step, 0)
+
+    barrier = pltpu.get_barrier_semaphore()
+    pl.semaphore_signal(
+        barrier, inc=1, device_id={"section": peer}, device_id_type=pl.DeviceIdType.MESH
+    )
+    load_g.start()
+    for c in range(chunks):
+        load_x(c).start()
+        load_v(c).start()
+    load_c.start()
+    load_b.start()
+    for c in range(chunks):
+        load_u(c).start()
+    pl.semaphore_wait(barrier, 1)
+
+    def project(source, arrive):
+        proj[...] = jnp.zeros_like(proj)
+        lg[...] = jnp.zeros_like(lg)
+
+        def body(c):
+            arrive(c)
+            part = source[c]
+            proj[...] += jnp.dot(part, vb[c], preferred_element_type=jnp.float32)
+            lg[...] += lax.dot_general(
+                part, gb[:, columns(c)], (((1,), (1,)), ((), ())),
+                preferred_element_type=jnp.float32,
+            )
+        each(body)
+
+    def mix():
+        logits = lg[...]
+        for e in range(experts):
+            first = jnp.tanh(proj[:, e * rank:(e + 1) * rank]).astype(jnp.bfloat16)
+            second = jnp.dot(first, cb[e], preferred_element_type=jnp.float32)
+            total = jnp.sum(jnp.exp(logits - logits[:, e:e + 1]), axis=1, keepdims=True)
+            gate = 1.0 / total
+            bl[:, e * rank:(e + 1) * rank] = (gate * jnp.tanh(second)).astype(jnp.bfloat16)
+
+    def crossed(c):
+        return (
+            jnp.dot(bl[...], ub[c], preferred_element_type=jnp.float32) + bb[:, columns(c)]
+        )
+
+    @pl.when(me == 0)
+    def _():
+        load_g.wait()
+
+        def loaded(c):
+            load_x(c).wait()
+            load_v(c).wait()
+
+        project(xb, loaded)
+        load_c.wait()
+        load_b.wait()
+        mix()
+
+        def own(c):
+            load_u(c).wait()
+            base = xb[c].astype(jnp.float32)
+            out1[c] = (base + base * crossed(c)).astype(jnp.bfloat16)
+            put(out1.at[c], in1, s1, r1, c).start()
+        each(own)
+        project(in1, lambda c: put(out1.at[c], in1, s1, r1, c).wait_recv())
+        mix()
+
+        def other(c):
+            base = in1[c].astype(jnp.float32)
+            out2[c] = (base + base * crossed(c)).astype(jnp.bfloat16)
+            put(out2.at[c], in2, s2, r2, c).start()
+        each(other)
+
+        def finish(c):
+            put(out2.at[c], in2, s2, r2, c).wait_recv()
+            ob[c] = (
+                out1[c].astype(jnp.float32)
+                + xb[c].astype(jnp.float32) * in2[c].astype(jnp.float32)
+            ).astype(jnp.bfloat16)
+            put_out(c).start()
+        each(finish)
+
+        def drain(c):
+            put(out1.at[c], in1, s1, r1, c).wait_send()
+            put(out2.at[c], in2, s2, r2, c).wait_send()
+            put_out(c).wait()
+        each(drain)
+
+    @pl.when(me == 1)
+    def _():
+        def send_x(c):
+            return put(x_hbm.at[:, columns(c)], in1, s1, r1, c)
+
+        each(lambda c: send_x(c).start())
+        load_g.wait()
+        load_c.wait()
+        load_b.wait()
+
+        def ready(c):
+            load_x(c).wait()
+            load_v(c).wait()
+            load_u(c).wait()
+        each(ready)
+        project(in1, lambda c: send_x(c).wait_recv())
+        mix()
+
+        def back(c):
+            out1[c] = crossed(c).astype(jnp.bfloat16)
+            put(out1.at[c], in2, s2, r2, c).start()
+        each(back)
+        project(in2, lambda c: put(out1.at[c], in2, s2, r2, c).wait_recv())
+        mix()
+
+        def finish(c):
+            ob[c] = (
+                in2[c].astype(jnp.float32) + xb[c].astype(jnp.float32) * crossed(c)
+            ).astype(jnp.bfloat16)
+            put_out(c).start()
+        each(finish)
+
+        def drain(c):
+            send_x(c).wait_send()
+            put(out1.at[c], in2, s2, r2, c).wait_send()
+            put_out(c).wait()
+        each(drain)
+
+
+def pair_device(features, in_proj, mix_proj, out_proj, gate_proj, cross_bias):
+    rows, depth = features.shape[2:]
+    experts, rank = mix_proj.shape[1:3]
+    inner = experts * rank
+    width = depth // CHUNKS
+    kind = jnp.bfloat16
+    block = pltpu.VMEM((CHUNKS, rows, width), kind)
+    sems = pltpu.SemaphoreType.DMA((CHUNKS,))
+    anywhere = pl.BlockSpec(memory_space=pl.ANY)
+    out = pl.pallas_call(
+        relay_kernel,
+        out_shape=jax.ShapeDtypeStruct((rows, depth), kind),
+        in_specs=[anywhere] * 6,
+        out_specs=anywhere,
+        scratch_shapes=[
+            block,
+            pltpu.VMEM((CHUNKS, width, inner), kind),
+            pltpu.VMEM((experts, rank, rank), kind),
+            pltpu.VMEM((CHUNKS, inner, width), kind),
+            pltpu.VMEM((experts, depth), kind),
+            pltpu.VMEM((1, depth), jnp.float32),
+            block, block, block, block, block,
+            pltpu.VMEM((rows, inner), jnp.float32),
+            pltpu.VMEM((rows, experts), jnp.float32),
+            pltpu.VMEM((rows, inner), kind),
+            sems, sems, sems, pltpu.SemaphoreType.DMA((3,)),
+            sems, sems, sems, sems, sems,
+        ],
+        compiler_params=pltpu.CompilerParams(
+            collective_id=0, has_side_effects=True, vmem_limit_bytes=60 * 1024 * 1024
+        ),
+    )(features[0, 0], in_proj[0], mix_proj[0], out_proj[0], gate_proj[0], cross_bias)
+    return out.reshape(features.shape)
 
 
 def from_behind(block, axis, distance):
@@ -112,8 +317,14 @@
         P("section", None, None),
         P("section", None),
     )
+    sections = mesh.shape["section"]
+
+    def choose(features, *weights):
+        whole = sections == 2 and features.shape[0] == 1 and features.shape[3] % 1024 == 0
+        return (pair_device if whole else per_device)(features, *weights)
+
     return jax.shard_map(
-        per_device,
+        choose,
         mesh=mesh,
         in_specs=placed,
         out_specs=P(None, "section", "dp", None),

time: 131 us -> 58.3 us (0.45)
  waiting for transfers between devices: 84.6 us -> 0 us
  Pallas kernels: 0 us -> 55.1 us
  matrix products: 14.5 us -> 0 us
  between operations: 13.5 us -> 0.01 us
  starting transfers between devices: 9.1 us -> 0 us
  other arithmetic: 8.06 us -> 0 us
  local copies, waits for them, and re-layouts: 0.26 us -> 2.29 us
    pallas_call x0 -> x1, Pallas kernels: none -> 55.1 us  [pair_device(): pl.pallas_call(relay_kernel, out_shape=jax.ShapeDtypeStruct((rows, depth)...]
    ppermute x3 -> x0, waiting for transfers between devices: 49.1 us -> none  [from_behind(): return lax.ppermute(block, axis, route)]
    all_gather x1 -> x0, waiting for transfers between devices: 34.9 us -> none  [per_device(): everyone = lax.all_gather(features, 'section', axis=1, tiled=True)]
    dot_general x8 -> x0, matrix products: 14.5 us -> none  [the longest x2 7.47 us: cross_layer(): crossed = jnp.dot(blended, u_mat, preferred_element_type=jnp.float32)]
    ppermute x3 -> x0, starting transfers between devices: 9.1 us -> none  [from_behind(): return lax.ppermute(block, axis, route)]
    select_n x4 -> x0, other arithmetic: 6.79 us -> none  [the longest x3 5.69 us: advance(): current = jnp.where(position == 0, anchor, incoming)]
    unnamed x6 -> x1, local copies, waits for them, and re-layouts: 0.01 us -> 2.29 us
  transfers between devices with their start and end apart: 4 -> 0, of which waited for: 3 -> 0; matrix products, arithmetic and copies ran while one was open for 9% -> 0% of each run, Pallas kernels for 0% -> 0%
where the time goes in v1:
time: 58.3 us; the launch traced here: 57.4 us
  Pallas kernels  55.1 us (95%)
  local copies, waits for them, and re-layouts  2.29 us (4%)
    pallas_call x1, Pallas kernels, pair_device(): pl.pallas_call(relay_kernel, out_shape=jax.ShapeDtypeStruct((rows, depth)...  55.1 us
    unnamed x1, local copies, waits for them, and re-layouts  2.29 us

profile of v1, /device:TPU:18, one launch (start us, length us, event | category | flops | bytes accessed | tf_op | source)
XLA Modules:
  0.0 57.4 jit_solution(16061144920885266916)
XLA Ops:
  0.0 55.1 %shard_map.64 = bf16[128,4096]{1,0:T(8,128)(2,1)} custom-call(bf16[128,4096]{1,0:T(8,128)(2,1)} %bitcast.9, bf16[4096,512]{1,0:T(8,128)(2,1)} %bitcast.6, bf16[2,256,256]{2,1,0:T(8,128)(2,1)} %bitcast.10, bf16[512,4096]{1,0:T(8,128)(2,1)} %bitcast.7, bf16[2,4096]{1,0:T(2,128)(2,1)} %bitcast.11, f32[1,4096]{1,0:T(1,128)} %b_hbm.1), custom_call_target="tpu_custom_call" | custom-call | tf_op jit(solution)/shard_map/pallas_call | solution.py:186
  55.1 2.3 %copy.8 = bf16[1,1,128,4096]{3,2,1,0:T(8,128)(2,1)} copy(bf16[1,1,128,4096]{3,2,1,0:T(8,128)(2,1)} %bitcast.8) | data formatting | bytes 2097152

commit v2 on v1

--- a/solution.py
+++ b/solution.py
@@ -1,23 +1,29 @@
 import jax
-
 import jax.numpy as jnp
 from jax import lax
 from jax.experimental import pallas as pl
 from jax.experimental.pallas import tpu as pltpu
 from jax.sharding import PartitionSpec as P
 
-CHUNKS = 8
+GROUP = 4
+MESH = pl.DeviceIdType.MESH
 
 
 def relay_kernel(
     x_hbm, v_hbm, c_hbm, u_hbm, g_hbm, b_hbm, o_hbm,
-    xb, vb, cb, ub, gb, bb, in1, in2, out1, out2, ob, proj, lg, bl,
-    lx, lv, lu, lw, s1, r1, s2, r2, so,
+    xb, vb, cb, ub, gb, bb, in1, out1, ob, gu, b2, proj, lg, bl, sent, got,
+    lx, lv, lu, lw, s1, r1, so, sx, rg, s_up, s_down, s_side, s_core, s3, r3,
 ):
     chunks, rows, width = xb.shape
     experts, rank, _ = cb.shape
+    layers = chunks // GROUP
     me = lax.axis_index("section")
     peer = 1 - me
+    mine = lax.axis_index("dp")
+    level = mine // GROUP
+    core = mine % 2
+    side = mine + 2 - 4 * (mine // 2 % 2)
+    twin = mine + 1 - 2 * core
 
     def columns(c):
         return pl.ds(pl.multiple_of(c * width, width), width)
@@ -35,110 +41,203 @@
     load_g = pltpu.make_async_copy(g_hbm, gb, lw.at[1])
     load_b = pltpu.make_async_copy(b_hbm, bb, lw.at[2])
 
-    def put(src, dst, send, recv, c):
+    def cross_over(src, dst, send, recv):
         return pltpu.make_async_remote_copy(
-            src_ref=src, dst_ref=dst.at[c], send_sem=send.at[c], recv_sem=recv.at[c],
-            device_id={"section": peer}, device_id_type=pl.DeviceIdType.MESH,
-        )
+            src_ref=src, dst_ref=dst, send_sem=send, recv_sem=recv,
+            device_id={"section": peer}, device_id_type=MESH,
+        )
+
+    def put(src, c):
+        return cross_over(src, in1.at[c], s1.at[c], r1.at[c])
 
     def put_out(c):
         return pltpu.make_async_copy(ob.at[c], o_hbm.at[:, columns(c)], so.at[c])
 
-    def each(body):
+    share_over = cross_over(u_hbm.at[:, columns(mine)], gu.at[mine], sx.at[0], rg.at[mine])
+    bias_over = cross_over(b_hbm, b2, s3.at[0], r3.at[0])
+    blend_over = cross_over(sent, got, s3.at[1], r3.at[1])
+
+    def hand(share, target, send):
+        return pltpu.make_async_remote_copy(
+            src_ref=gu.at[share], dst_ref=gu.at[share], send_sem=send.at[share],
+            recv_sem=rg.at[share], device_id={"dp": target}, device_id_type=MESH,
+        )
+
+    def await_share(share):
+        hand(share, side, s_side).wait_recv()
+
+    def pass_on(copy, finish):
+        if finish:
+            copy.wait_send()
+        else:
+            copy.start()
+
+    def along(share, go_up, go_down, finish):
+        if go_up:
+            @pl.when(level < layers - 1)
+            def _():
+                pass_on(hand(share, mine + GROUP, s_up), finish)
+        if go_down:
+            @pl.when(level > 0)
+            def _():
+                pass_on(hand(share, mine - GROUP, s_down), finish)
+        pass_on(hand(share, side, s_side), finish)
+        pass_on(hand(share, twin, s_core), finish)
+
+    def line_event(d, finish=False):
+        def act(share, go_up, go_down):
+            if not finish:
+                await_share(share)
+            along(share, go_up, go_down, finish)
+        if d == 0:
+            act(mine, True, True)
+            return
+        pl.when(level >= d)(lambda: act(mine - GROUP * d, True, False))
+        pl.when(level + d < layers)(lambda: act(mine + GROUP * d, False, True))
+
+    def side_event(d, finish=False):
+        def act(share):
+            if not finish:
+                await_share(share)
+            pass_on(hand(share, twin, s_core), finish)
+        if d == 0:
+            act(side)
+            return
+        pl.when(level >= d)(lambda: act(side - GROUP * d))
+        pl.when(level + d < layers)(lambda: act(side + GROUP * d))
+
+    def each(body, start=0, stop=chunks):
         def step(c, carry):
             body(c)
             return carry
-        lax.fori_loop(0, chunks, step, 0)
+        lax.fori_loop(start, stop, step, 0)
 
     barrier = pltpu.get_barrier_semaphore()
-    pl.semaphore_signal(
-        barrier, inc=1, device_id={"section": peer}, device_id_type=pl.DeviceIdType.MESH
-    )
+    pl.semaphore_signal(barrier, inc=1, device_id={"section": peer}, device_id_type=MESH)
+    pl.semaphore_signal(barrier, inc=1, device_id={"dp": side}, device_id_type=MESH)
+    pl.semaphore_signal(barrier, inc=1, device_id={"dp": twin}, device_id_type=MESH)
+
+    @pl.when(level < layers - 1)
+    def _():
+        pl.semaphore_signal(barrier, inc=1, device_id={"dp": mine + GROUP}, device_id_type=MESH)
+
+    @pl.when(level > 0)
+    def _():
+        pl.semaphore_signal(barrier, inc=1, device_id={"dp": mine - GROUP}, device_id_type=MESH)
+
     load_g.start()
-    for c in range(chunks):
+
+    def load_first(c):
         load_x(c).start()
         load_v(c).start()
+    each(load_first)
     load_c.start()
     load_b.start()
-    for c in range(chunks):
-        load_u(c).start()
-    pl.semaphore_wait(barrier, 1)
-
-    def project(source, arrive):
+    each(lambda c: load_u(c).start())
+    inside = (level > 0) & (level < layers - 1)
+
+    @pl.when(inside)
+    def _():
+        pl.semaphore_wait(barrier, 5)
+
+    @pl.when(jnp.logical_not(inside))
+    def _():
+        pl.semaphore_wait(barrier, 4 if layers > 1 else 3)
+
+    share_over.start()
+    bias_over.start()
+
+    def clear():
         proj[...] = jnp.zeros_like(proj)
         lg[...] = jnp.zeros_like(lg)
 
-        def body(c):
-            arrive(c)
-            part = source[c]
-            proj[...] += jnp.dot(part, vb[c], preferred_element_type=jnp.float32)
-            lg[...] += lax.dot_general(
-                part, gb[:, columns(c)], (((1,), (1,)), ((), ())),
-                preferred_element_type=jnp.float32,
-            )
-        each(body)
-
-    def mix():
+    def gather_in(part, c):
+        proj[...] += jnp.dot(part, vb[c], preferred_element_type=jnp.float32)
+        lg[...] += lax.dot_general(
+            part, gb[:, columns(c)], (((1,), (1,)), ((), ())),
+            preferred_element_type=jnp.float32,
+        )
+
+    def mix(target):
         logits = lg[...]
         for e in range(experts):
             first = jnp.tanh(proj[:, e * rank:(e + 1) * rank]).astype(jnp.bfloat16)
             second = jnp.dot(first, cb[e], preferred_element_type=jnp.float32)
             total = jnp.sum(jnp.exp(logits - logits[:, e:e + 1]), axis=1, keepdims=True)
             gate = 1.0 / total
-            bl[:, e * rank:(e + 1) * rank] = (gate * jnp.tanh(second)).astype(jnp.bfloat16)
-
-    def crossed(c):
+            target[:, e * rank:(e + 1) * rank] = (gate * jnp.tanh(second)).astype(jnp.bfloat16)
+
+    def crossed(blend, maps, shift, c):
         return (
-            jnp.dot(bl[...], ub[c], preferred_element_type=jnp.float32) + bb[:, columns(c)]
-        )
+            jnp.dot(blend[...], maps[c], preferred_element_type=jnp.float32)
+            + shift[:, columns(c)]
+        )
+
+    def relay(wait_chunk):
+        line_event(0)
+        clear()
+        marks = [0] + [chunks * (d + 1) // layers - chunks // (2 * layers) for d in range(layers - 1)]
+        marks += [chunks]
+
+        def body(c):
+            wait_chunk(c)
+            gather_in(in1[c], c)
+
+        for d in range(layers):
+            if d == 1 or d > 1 and d < layers - 1:
+                line_event(d)
+            if 1 <= d < layers - 1:
+                side_event(d - 1)
+            each(body, marks[d], marks[d + 1])
+        mix(sent)
+        blend_over.start()
+        if layers > 1:
+            line_event(layers - 1)
+        for d in range(max(layers - 2, 0), layers):
+            side_event(d)
+
+    def take_share(c):
+        @pl.when(c % 2 != core)
+        def _():
+            await_share(c)
 
     @pl.when(me == 0)
     def _():
         load_g.wait()
-
-        def loaded(c):
+        clear()
+
+        def first(c):
             load_x(c).wait()
             load_v(c).wait()
-
-        project(xb, loaded)
+            gather_in(xb[c], c)
+        each(first)
         load_c.wait()
         load_b.wait()
-        mix()
+        mix(bl)
 
         def own(c):
             load_u(c).wait()
             base = xb[c].astype(jnp.float32)
-            out1[c] = (base + base * crossed(c)).astype(jnp.bfloat16)
-            put(out1.at[c], in1, s1, r1, c).start()
+            out1[c] = (base + base * crossed(bl, ub, bb, c)).astype(jnp.bfloat16)
+            put(out1.at[c], c).start()
         each(own)
-        project(in1, lambda c: put(out1.at[c], in1, s1, r1, c).wait_recv())
-        mix()
-
-        def other(c):
-            base = in1[c].astype(jnp.float32)
-            out2[c] = (base + base * crossed(c)).astype(jnp.bfloat16)
-            put(out2.at[c], in2, s2, r2, c).start()
-        each(other)
+        relay(lambda c: put(out1.at[c], c).wait_recv())
+        bias_over.wait_recv()
+        blend_over.wait_recv()
 
         def finish(c):
-            put(out2.at[c], in2, s2, r2, c).wait_recv()
+            take_share(c)
             ob[c] = (
                 out1[c].astype(jnp.float32)
-                + xb[c].astype(jnp.float32) * in2[c].astype(jnp.float32)
+                + xb[c].astype(jnp.float32) * crossed(got, gu, b2, c)
             ).astype(jnp.bfloat16)
             put_out(c).start()
         each(finish)
 
-        def drain(c):
-            put(out1.at[c], in1, s1, r1, c).wait_send()
-            put(out2.at[c], in2, s2, r2, c).wait_send()
-            put_out(c).wait()
-        each(drain)
-
     @pl.when(me == 1)
     def _():
         def send_x(c):
-            return put(x_hbm.at[:, columns(c)], in1, s1, r1, c)
+            return put(x_hbm.at[:, columns(c)], c)
 
         each(lambda c: send_x(c).start())
         load_g.wait()
@@ -150,38 +249,51 @@
             load_v(c).wait()
             load_u(c).wait()
         each(ready)
-        project(in1, lambda c: send_x(c).wait_recv())
-        mix()
-
-        def back(c):
-            out1[c] = crossed(c).astype(jnp.bfloat16)
-            put(out1.at[c], in2, s2, r2, c).start()
-        each(back)
-        project(in2, lambda c: put(out1.at[c], in2, s2, r2, c).wait_recv())
-        mix()
+        relay(lambda c: send_x(c).wait_recv())
+        bias_over.wait_recv()
+        blend_over.wait_recv()
+        clear()
+
+        def advance(c):
+            take_share(c)
+            base = xb[c].astype(jnp.float32)
+            after = (base + base * crossed(got, gu, b2, c)).astype(jnp.bfloat16)
+            out1[c] = after
+            gather_in(after, c)
+        each(advance)
+        mix(bl)
 
         def finish(c):
             ob[c] = (
-                in2[c].astype(jnp.float32) + xb[c].astype(jnp.float32) * crossed(c)
+                out1[c].astype(jnp.float32)
+                + xb[c].astype(jnp.float32) * crossed(bl, ub, bb, c)
             ).astype(jnp.bfloat16)
             put_out(c).start()
         each(finish)
 
-        def drain(c):
-            send_x(c).wait_send()
-            put(out1.at[c], in2, s2, r2, c).wait_send()
-            put_out(c).wait()
-        each(drain)
+    def drain(c):
+        put(out1.at[c], c).wait_send()
+        put_out(c).wait()
+    each(drain)
+    share_over.wait_send()
+    bias_over.wait_send()
+    blend_over.wait_send()
+    for d in range(layers):
+        line_event(d, True)
+        side_event(d, True)
 
 
 def pair_device(features, in_proj, mix_proj, out_proj, gate_proj, cross_bias):
     rows, depth = features.shape[2:]
     experts, rank = mix_proj.shape[1:3]
     inner = experts * rank
-    width = depth // CHUNKS
+    chunks = lax.axis_size("dp")
+    width = depth // chunks
     kind = jnp.bfloat16
-    block = pltpu.VMEM((CHUNKS, rows, width), kind)
-    sems = pltpu.SemaphoreType.DMA((CHUNKS,))
+    block = pltpu.VMEM((chunks, rows, width), kind)
+    blend = pltpu.VMEM((rows, inner), kind)
+    sems = pltpu.SemaphoreType.DMA((chunks,))
+    two = pltpu.SemaphoreType.DMA((2,))
     anywhere = pl.BlockSpec(memory_space=pl.ANY)
     out = pl.pallas_call(
         relay_kernel,
@@ -190,17 +302,20 @@
         out_specs=anywhere,
         scratch_shapes=[
             block,
-            pltpu.VMEM((CHUNKS, width, inner), kind),
+            pltpu.VMEM((chunks, width, inner), kind),
             pltpu.VMEM((experts, rank, rank), kind),
-            pltpu.VMEM((CHUNKS, inner, width), kind),
+            pltpu.VMEM((chunks, inner, width), kind),
             pltpu.VMEM((experts, depth), kind),
             pltpu.VMEM((1, depth), jnp.float32),
-            block, block, block, block, block,
+            block, block, block,
+            pltpu.VMEM((chunks, inner, width), kind),
+            pltpu.VMEM((1, depth), jnp.float32),
             pltpu.VMEM((rows, inner), jnp.float32),
             pltpu.VMEM((rows, experts), jnp.float32),
-            pltpu.VMEM((rows, inner), kind),
+            blend, blend, blend,
             sems, sems, sems, pltpu.SemaphoreType.DMA((3,)),
-            sems, sems, sems, sems, sems,
+            sems, sems, sems,
+            two, sems, sems, sems, sems, sems, two, two,
         ],
         compiler_params=pltpu.CompilerParams(
             collective_id=0, has_side_effects=True, vmem_limit_bytes=60 * 1024 * 1024
@@ -317,10 +432,11 @@
         P("section", None, None),
         P("section", None),
     )
-    sections = mesh.shape["section"]
+    sections, groups = mesh.shape["section"], mesh.shape["dp"]
 
     def choose(features, *weights):
-        whole = sections == 2 and features.shape[0] == 1 and features.shape[3] % 1024 == 0
+        whole = sections == 2 and features.shape[0] == 1 and groups % GROUP == 0
+        whole = whole and features.shape[3] % (groups * 128) == 0
         return (pair_device if whole else per_device)(features, *weights)
 
     return jax.shard_map(

time: 58.3 us -> 53.9 us (0.925)
  the two profiles are of different devices: /device:TPU:18 before, /device:TPU:27 now
where the time goes in v2:
time: 53.9 us; the launch traced here: 53.7 us
  Pallas kernels  51.4 us (95%)
  local copies, waits for them, and re-layouts  2.29 us (4%)
    pallas_call x1, Pallas kernels, pair_device(): pl.pallas_call(relay_kernel, out_shape=jax.ShapeDtypeStruct((rows, depth)...  51.4 us
    unnamed x1, local copies, waits for them, and re-layouts  2.29 us

profile of v2, /device:TPU:27, one launch (start us, length us, event | category | flops | bytes accessed | tf_op | source)
XLA Modules:
  0.0 53.7 jit_solution(15734936622986438196)
XLA Ops:
  0.0 51.4 %shard_map.64 = bf16[128,4096]{1,0:T(8,128)(2,1)} custom-call(bf16[128,4096]{1,0:T(8,128)(2,1)} %bitcast.9, bf16[4096,512]{1,0:T(8,128)(2,1)} %bitcast.6, bf16[2,256,256]{2,1,0:T(8,128)(2,1)} %bitcast.10, bf16[512,4096]{1,0:T(8,128)(2,1)} %bitcast.7, bf16[2,4096]{1,0:T(2,128)(2,1)} %bitcast.11, f32[1,4096]{1,0:T(1,128)} %b_hbm.1), custom_call_target="tpu_custom_call" | custom-call | tf_op jit(solution)/shard_map/pallas_call | solution.py:298
  51.4 2.3 %copy.8 = bf16[1,1,128,4096]{3,2,1,0:T(8,128)(2,1)} copy(bf16[1,1,128,4096]{3,2,1,0:T(8,128)(2,1)} %bitcast.8) | data formatting | bytes 2097152

commit v3 on v2

--- a/solution.py
+++ b/solution.py
@@ -6,7 +6,10 @@
 from jax.sharding import PartitionSpec as P
 
 GROUP = 4
+BATCH = 8
 MESH = pl.DeviceIdType.MESH
+LINE_AT = lambda d, chunks, layers: d * (d + 1) // 2 * chunks // 16 if d < layers - 1 else chunks - 2
+SIDE_AT = lambda d, chunks, layers: (4 * d + 2) * chunks // 16 if d < layers - 2 else chunks - 2 if d < layers - 1 else chunks + 1
 
 
 def relay_kernel(
@@ -112,6 +115,12 @@
             return carry
         lax.fori_loop(start, stop, step, 0)
 
+    def batches(body):
+        def step(i, carry):
+            body([i * BATCH + j for j in range(BATCH)])
+            return carry
+        lax.fori_loop(0, chunks // BATCH, step, 0)
+
     barrier = pltpu.get_barrier_semaphore()
     pl.semaphore_signal(barrier, inc=1, device_id={"section": peer}, device_id_type=MESH)
     pl.semaphore_signal(barrier, inc=1, device_id={"dp": side}, device_id_type=MESH)
@@ -151,11 +160,14 @@
         proj[...] = jnp.zeros_like(proj)
         lg[...] = jnp.zeros_like(lg)
 
-    def gather_in(part, c):
-        proj[...] += jnp.dot(part, vb[c], preferred_element_type=jnp.float32)
-        lg[...] += lax.dot_general(
-            part, gb[:, columns(c)], (((1,), (1,)), ((), ())),
-            preferred_element_type=jnp.float32,
+    def gather_in(parts, cs):
+        both = (((1,), (1,)), ((), ()))
+        proj[...] += sum(
+            jnp.dot(part, vb[c], preferred_element_type=jnp.float32) for part, c in zip(parts, cs)
+        )
+        lg[...] += sum(
+            lax.dot_general(part, gb[:, columns(c)], both, preferred_element_type=jnp.float32)
+            for part, c in zip(parts, cs)
         )
 
     def mix(target):
@@ -174,27 +186,31 @@
         )
 
     def relay(wait_chunk):
-        line_event(0)
+        plan = {}
+        for d in range(layers):
+            plan.setdefault(LINE_AT(d, chunks, layers), []).append((line_event, d))
+            plan.setdefault(SIDE_AT(d, chunks, layers), []).append((side_event, d))
         clear()
-        marks = [0] + [chunks * (d + 1) // layers - chunks // (2 * layers) for d in range(layers - 1)]
-        marks += [chunks]
 
         def body(c):
             wait_chunk(c)
-            gather_in(in1[c], c)
-
-        for d in range(layers):
-            if d == 1 or d > 1 and d < layers - 1:
-                line_event(d)
-            if 1 <= d < layers - 1:
-                side_event(d - 1)
-            each(body, marks[d], marks[d + 1])
+            gather_in([in1[c]], [c])
+
+        at = 0
+        for mark in sorted(plan):
+            if mark > chunks:
+                break
+            each(body, at, mark)
+            at = mark
+            for event, d in plan[mark]:
+                event(d)
+        each(body, at, chunks)
         mix(sent)
         blend_over.start()
-        if layers > 1:
-            line_event(layers - 1)
-        for d in range(max(layers - 2, 0), layers):
-            side_event(d)
+        for mark in sorted(plan):
+            if mark > chunks:
+                for event, d in plan[mark]:
+                    event(d)
 
     def take_share(c):
         @pl.when(c % 2 != core)
@@ -206,11 +222,12 @@
         load_g.wait()
         clear()
 
-        def first(c):
-            load_x(c).wait()
-            load_v(c).wait()
-            gather_in(xb[c], c)
-        each(first)
+        def first(cs):
+            for c in cs:
+                load_x(c).wait()
+                load_v(c).wait()
+            gather_in([xb[c] for c in cs], cs)
+        batches(first)
         load_c.wait()
         load_b.wait()
         mix(bl)
@@ -225,14 +242,17 @@
         bias_over.wait_recv()
         blend_over.wait_recv()
 
-        def finish(c):
-            take_share(c)
-            ob[c] = (
-                out1[c].astype(jnp.float32)
-                + xb[c].astype(jnp.float32) * crossed(got, gu, b2, c)
-            ).astype(jnp.bfloat16)
-            put_out(c).start()
-        each(finish)
+        each(take_share)
+
+        def finish(cs):
+            for c in cs:
+                ob[c] = (
+                    out1[c].astype(jnp.float32)
+                    + xb[c].astype(jnp.float32) * crossed(got, gu, b2, c)
+                ).astype(jnp.bfloat16)
+            for c in cs:
+                put_out(c).start()
+        batches(finish)
 
     @pl.when(me == 1)
     def _():
@@ -254,22 +274,28 @@
         blend_over.wait_recv()
         clear()
 
-        def advance(c):
-            take_share(c)
-            base = xb[c].astype(jnp.float32)
-            after = (base + base * crossed(got, gu, b2, c)).astype(jnp.bfloat16)
-            out1[c] = after
-            gather_in(after, c)
-        each(advance)
+        each(take_share)
+
+        def advance(cs):
+            parts = []
+            for c in cs:
+                base = xb[c].astype(jnp.float32)
+                parts.append((base + base * crossed(got, gu, b2, c)).astype(jnp.bfloat16))
+            for c, part in zip(cs, parts):
+                out1[c] = part
+            gather_in(parts, cs)
+        batches(advance)
         mix(bl)
 
-        def finish(c):
-            ob[c] = (
-                out1[c].astype(jnp.float32)
-                + xb[c].astype(jnp.float32) * crossed(bl, ub, bb, c)
-            ).astype(jnp.bfloat16)
-            put_out(c).start()
-        each(finish)
+        def finish(cs):
+            for c in cs:
+                ob[c] = (
+                    out1[c].astype(jnp.float32)
+                    + xb[c].astype(jnp.float32) * crossed(bl, ub, bb, c)
+                ).astype(jnp.bfloat16)
+            for c in cs:
+                put_out(c).start()
+        batches(finish)
 
     def drain(c):
         put(out1.at[c], c).wait_send()
@@ -435,7 +461,7 @@
     sections, groups = mesh.shape["section"], mesh.shape["dp"]
 
     def choose(features, *weights):
-        whole = sections == 2 and features.shape[0] == 1 and groups % GROUP == 0
+        whole = sections == 2 and features.shape[0] == 1 and groups % BATCH == 0
         whole = whole and features.shape[3] % (groups * 128) == 0
         return (pair_device if whole else per_device)(features, *weights)
 

time: 53.9 us -> 45.4 us (0.84)
  the two profiles are of different devices: /device:TPU:27 before, /device:TPU:18 now
where the time goes in v3:
time: 45.4 us; the launch traced here: 45.2 us
  Pallas kernels  42.9 us (94%)
  local copies, waits for them, and re-layouts  2.29 us (5%)
    pallas_call x1, Pallas kernels, pair_device(): pl.pallas_call(relay_kernel, out_shape=jax.ShapeDtypeStruct((rows, depth)...  42.9 us
    unnamed x1, local copies, waits for them, and re-layouts  2.29 us

profile of v3, /device:TPU:18, one launch (start us, length us, event | category | flops | bytes accessed | tf_op | source)
XLA Modules:
  0.0 45.2 jit_solution(17241800303691902150)
XLA Ops:
  0.0 42.9 %shard_map.64 = bf16[128,4096]{1,0:T(8,128)(2,1)} custom-call(bf16[128,4096]{1,0:T(8,128)(2,1)} %bitcast.9, bf16[4096,512]{1,0:T(8,128)(2,1)} %bitcast.6, bf16[2,256,256]{2,1,0:T(8,128)(2,1)} %bitcast.10, bf16[512,4096]{1,0:T(8,128)(2,1)} %bitcast.7, bf16[2,4096]{1,0:T(2,128)(2,1)} %bitcast.11, f32[1,4096]{1,0:T(1,128)} %b_hbm.1), custom_call_target="tpu_custom_call" | custom-call | tf_op jit(solution)/shard_map/pallas_call | solution.py:324
  42.9 2.3 %copy.8 = bf16[1,1,128,4096]{3,2,1,0:T(8,128)(2,1)} copy(bf16[1,1,128,4096]{3,2,1,0:T(8,128)(2,1)} %bitcast.8) | data formatting | bytes 2097152

commit v4 on v3

--- a/solution.py
+++ b/solution.py
@@ -58,7 +58,10 @@
 
     share_over = cross_over(u_hbm.at[:, columns(mine)], gu.at[mine], sx.at[0], rg.at[mine])
     bias_over = cross_over(b_hbm, b2, s3.at[0], r3.at[0])
-    blend_over = cross_over(sent, got, s3.at[1], r3.at[1])
+
+    def blend_over(e):
+        part = (slice(None), pl.ds(e * rank, rank))
+        return cross_over(sent.at[part], got.at[part], s3.at[1 + e], r3.at[1 + e])
 
     def hand(share, target, send):
         return pltpu.make_async_remote_copy(
@@ -170,7 +173,7 @@
             for part, c in zip(parts, cs)
         )
 
-    def mix(target):
+    def mix(target, after=None):
         logits = lg[...]
         for e in range(experts):
             first = jnp.tanh(proj[:, e * rank:(e + 1) * rank]).astype(jnp.bfloat16)
@@ -178,6 +181,8 @@
             total = jnp.sum(jnp.exp(logits - logits[:, e:e + 1]), axis=1, keepdims=True)
             gate = 1.0 / total
             target[:, e * rank:(e + 1) * rank] = (gate * jnp.tanh(second)).astype(jnp.bfloat16)
+            if after is not None:
+                after(e)
 
     def crossed(blend, maps, shift, c):
         return (
@@ -205,8 +210,7 @@
             for event, d in plan[mark]:
                 event(d)
         each(body, at, chunks)
-        mix(sent)
-        blend_over.start()
+        mix(sent, lambda e: blend_over(e).start())
         for mark in sorted(plan):
             if mark > chunks:
                 for event, d in plan[mark]:
@@ -240,7 +244,8 @@
         each(own)
         relay(lambda c: put(out1.at[c], c).wait_recv())
         bias_over.wait_recv()
-        blend_over.wait_recv()
+        for e in range(experts):
+            blend_over(e).wait_recv()
 
         each(take_share)
 
@@ -271,7 +276,8 @@
         each(ready)
         relay(lambda c: send_x(c).wait_recv())
         bias_over.wait_recv()
-        blend_over.wait_recv()
+        for e in range(experts):
+            blend_over(e).wait_recv()
         clear()
 
         each(take_share)
@@ -303,7 +309,8 @@
     each(drain)
     share_over.wait_send()
     bias_over.wait_send()
-    blend_over.wait_send()
+    for e in range(experts):
+        blend_over(e).wait_send()
     for d in range(layers):
         line_event(d, True)
         side_event(d, True)
@@ -320,6 +327,7 @@
     blend = pltpu.VMEM((rows, inner), kind)
     sems = pltpu.SemaphoreType.DMA((chunks,))
     two = pltpu.SemaphoreType.DMA((2,))
+    extra = pltpu.SemaphoreType.DMA((1 + experts,))
     anywhere = pl.BlockSpec(memory_space=pl.ANY)
     out = pl.pallas_call(
         relay_kernel,
@@ -341,7 +349,7 @@
             blend, blend, blend,
             sems, sems, sems, pltpu.SemaphoreType.DMA((3,)),
             sems, sems, sems,
-            two, sems, sems, sems, sems, sems, two, two,
+            two, sems, sems, sems, sems, sems, extra, extra,
         ],
         compiler_params=pltpu.CompilerParams(
             collective_id=0, has_side_effects=True, vmem_limit_bytes=60 * 1024 * 1024

time: 45.4 us -> 45.3 us (level)
  no operation moved by 1% of the time
where the time goes in v4:
time: 45.3 us; the launch traced here: 45.2 us
  Pallas kernels  42.9 us (95%)
  local copies, waits for them, and re-layouts  2.29 us (5%)
    pallas_call x1, Pallas kernels, pair_device(): pl.pallas_call(relay_kernel, out_shape=jax.ShapeDtypeStruct((rows, depth)...  42.9 us
    unnamed x1, local copies, waits for them, and re-layouts  2.29 us

profile of v4, /device:TPU:18, one launch (start us, length us, event | category | flops | bytes accessed | tf_op | source)
XLA Modules:
  0.0 45.2 jit_solution(5220163384992044661)
XLA Ops:
  0.0 42.9 %shard_map.64 = bf16[128,4096]{1,0:T(8,128)(2,1)} custom-call(bf16[128,4096]{1,0:T(8,128)(2,1)} %bitcast.9, bf16[4096,512]{1,0:T(8,128)(2,1)} %bitcast.6, bf16[2,256,256]{2,1,0:T(8,128)(2,1)} %bitcast.10, bf16[512,4096]{1,0:T(8,128)(2,1)} %bitcast.7, bf16[2,4096]{1,0:T(2,128)(2,1)} %bitcast.11, f32[1,4096]{1,0:T(1,128)} %b_hbm.1), custom_call_target="tpu_custom_call" | custom-call | tf_op jit(solution)/shard_map/pallas_call | solution.py:332
  42.9 2.3 %copy.8 = bf16[1,1,128,4096]{3,2,1,0:T(8,128)(2,1)} copy(bf16[1,1,128,4096]{3,2,1,0:T(8,128)(2,1)} %bitcast.8) | data formatting | bytes 2097152
